TPU v7x, 32 devices: a whole 2x2x4 slice. The times are simulated.
32 devices in a mesh: expert: 4 (over x, core), shard: 8 (over z, y).
Axes of the slice: x: 2, y: 2, z: 4, core: 2. Of those that a mesh axis runs over, the one named last changes fastest.
Arguments:
- master_gate: float32 [64, 2048, 1024], P('expert', 'shard'), may hold values from -0.1875 to 0.1875
- second_gate: bfloat16 [64, 2048, 1024], P('expert', 'shard'), may hold values from -0.0625 to 0.0625
- master_up: float32 [64, 2048, 1024], P('expert', 'shard'), may hold values from -0.1875 to 0.1875
- second_up: bfloat16 [64, 2048, 1024], P('expert', 'shard'), may hold values from -0.0625 to 0.0625
- master_down: float32 [64, 1024, 2048], P('expert', None, 'shard'), may hold values from -0.25 to 0.25
- second_down: bfloat16 [64, 1024, 2048], P('expert', None, 'shard'), may hold values from -0.09375 to 0.09375
- router_weight: float32 [2048, 64], P('shard', 'expert'), may hold values from -0.125 to 0.125
- router_gain: float32 [2048], P('shard'), may hold values from 0.25 to 1.75
Outputs:
- final_gate: bfloat16 [64, 2048, 1024], P('expert', None, 'shard')
- final_up: bfloat16 [64, 2048, 1024], P('expert', None, 'shard')
- final_down: bfloat16 [64, 1024, 2048], P('expert', 'shard')
- scale_gate: float32 [64, 1024], P('expert', 'shard')
- scale_up: float32 [64, 1024], P('expert', 'shard')
- scale_down: float32 [64, 1024], P('expert', 'shard')
- serve_router: bfloat16 [2048, 64], replicated
All inputs are finite; a program needn't handle non-finite values. Where the computation divides by a largest or mean magnitude, that divisor is 1e-20 or more.
Results may differ from a plain program's by a relative error of at most 0.001.
Values may be sent and summed in bfloat16 or wider, within the bound.
A program may use at most 192 MiB of HBM per device.

v0:
```python
import jax
import jax.numpy as jnp
from jax import lax
from jax.sharding import PartitionSpec as P


def per_device(
    master_gate,
    second_gate,
    master_up,
    second_up,
    master_down,
    second_down,
    router_weight,
    router_gain,
):
    merged_gate = master_gate + second_gate.astype(jnp.float32)
    merged_up = master_up + second_up.astype(jnp.float32)
    merged_down = master_down + second_down.astype(jnp.float32)
    scale_gate, scale_up, scale_down = lax.pmax(
        (
            jnp.max(jnp.abs(merged_gate), axis=1),
            jnp.max(jnp.abs(merged_up), axis=1),
            jnp.max(jnp.abs(merged_down), axis=2),
        ),
        "shard",
    )
    narrow_gate, narrow_up, narrow_down = (
        (merged_gate / jnp.expand_dims(scale_gate, 1)).astype(jnp.bfloat16),
        (merged_up / jnp.expand_dims(scale_up, 1)).astype(jnp.bfloat16),
        (merged_down / jnp.expand_dims(scale_down, 2)).astype(jnp.bfloat16),
    )
    final_gate, final_up = (
        lax.all_to_all(narrow_gate, "shard", split_axis=2, concat_axis=1, tiled=True),
        lax.all_to_all(narrow_up, "shard", split_axis=2, concat_axis=1, tiled=True),
    )
    final_down = lax.all_to_all(narrow_down, "shard", split_axis=1, concat_axis=2, tiled=True)
    scale_gate = lax.dynamic_slice_in_dim(
        scale_gate, lax.axis_index("shard") * final_gate.shape[2], final_gate.shape[2], axis=1
    )
    scale_up = lax.dynamic_slice_in_dim(
        scale_up, lax.axis_index("shard") * final_up.shape[2], final_up.shape[2], axis=1
    )
    scale_down = lax.dynamic_slice_in_dim(
        scale_down, lax.axis_index("shard") * final_down.shape[1], final_down.shape[1], axis=1
    )
    part_router = (router_weight * router_gain[:, None]).astype(jnp.bfloat16)
    row_router = lax.all_gather(part_router, "shard", axis=0, tiled=True)
    serve_router = lax.all_gather(row_router, "expert", axis=1, tiled=True)
    return (final_gate, final_up, final_down, scale_gate, scale_up, scale_down, serve_router)


def solution(mesh):
    in_specs = (
        P("expert", "shard", None),
        P("expert", "shard", None),
        P("expert", "shard", None),
        P("expert", "shard", None),
        P("expert", None, "shard"),
        P("expert", None, "shard"),
        P("shard", "expert"),
        P("shard"),
    )
    out_specs = (
        P("expert", None, "shard"),
        P("expert", None, "shard"),
        P("expert", "shard", None),
        P("expert", "shard"),
        P("expert", "shard"),
        P("expert", "shard"),
        P(),
    )
    return jax.shard_map(
        per_device, mesh=mesh, in_specs=in_specs, out_specs=out_specs, check_vma=False
    )
```

profile of v0, /device:TPU:0, one launch (start us, length us, event | category | flops | bytes accessed | tf_op | source)
XLA Modules:
  0.0 877.2 jit_solution(5564650451525219035)
XLA Ops:
  7.2 0.0 all-reduce.3.cloned.1.call-start
  7.2 17.6 %copy.34 = f32[16,256,1024]{1,0,2:T(8,128)} copy(f32[16,256,1024]{2,1,0:T(8,128)} %param.10) | data formatting | bytes 33554432 | tf_op args[2]
  24.8 12.5 %copy.33 = bf16[16,256,1024]{1,0,2:T(8,128)(2,1)} copy(bf16[16,256,1024]{2,1,0:T(8,128)(2,1)} %param.11) | data formatting | bytes 16777216 | tf_op args[3]
  37.3 17.6 %copy.31 = f32[16,256,1024]{1,0,2:T(8,128)} copy(f32[16,256,1024]{2,1,0:T(8,128)} %param.8) | data formatting | bytes 33554432 | tf_op args[0]
  54.9 12.5 %copy.30 = bf16[16,256,1024]{1,0,2:T(8,128)(2,1)} copy(bf16[16,256,1024]{2,1,0:T(8,128)(2,1)} %param.9) | data formatting | bytes 16777216 | tf_op args[1]
  67.4 11.1 %abs_reduce_fusion.1 = f32[16,1024]{0,1:T(8,128)} fusion(f32[16,256,1024]{1,0,2:T(8,128)} %copy.34, bf16[16,256,1024]{1,0,2:T(8,128)(2,1)} %copy.33), kind=kLoop, calls=%fused_computation.4 | loop fusion | flops 16760832 | bytes 25231360 | tf_op jit(solution)/shard_map/reduce_max | solution.py:23
  78.5 2.1 copy-done
  80.6 2.4 copy-done.1
  83.0 4.3 abs_reduce_fusion.2
  87.3 29.3 %abs_reduce_fusion = f32[16,1024]{0,1:T(8,128)} fusion(f32[16,1024,256]{2,1,0:T(8,128)} %param.12, bf16[16,1024,256]{2,1,0:T(8,128)(2,1)S(1)} %bitcast.14), kind=kLoop, calls=%fused_computation.2 | loop fusion | flops 16760832 | bytes 25231360 | tf_op jit(solution)/shard_map/reduce_max | solution.py:24
  116.5 0.0 all-reduce.3.cloned.1.call-update
  116.6 92.5 %all-reduce.3.cloned.1.call-done = (f32[16,1024]{0,1:T(8,128)}, f32[16,1024]{0,1:T(8,128)}, f32[16,1024]{0,1:T(8,128)}) async-done(((f32[16,1024]{0,1:T(8,128)}, f32[16,1024]{0,1:T(8,128)}, f32[16,1024]{0,1:T(8,128)}), (f32[16,1024]{0,1:T(8,128)}, f32[16,1024]{0,1:T(8,128)}, f32[16,1024]{0,1:T(8,128)})) %all-reduce.3.cloned.1.call-update) | async-done | bytes 196624 | tf_op jit(solution)/shard_map/pmax | solution.py:20
  209.0 20.5 %divide_convert_fusion.1 = (bf16[16,256,1024]{1,0,2:T(8,128)(2,1)}, bf16[16,256,1024]{1,0,2:T(8,128)(2,1)S(1)}) fusion(f32[16,256,1024]{1,0,2:T(8,128)} %copy.34, bf16[16,256,1024]{1,0,2:T(8,128)(2,1)} %copy.33, f32[16,1024]{0,1:T(8,128)} %get-tuple-element.15, f32[16,1024]{0,1:T(8,128)} %get-tuple-element.14, f32[16,256,1024]{1,0,2:T(8,128)} %copy.31, ...), kind=kLoop, calls=%fused_computation.3 | loop fusion | flops 33554432 | bytes 67239936 | tf_op jit(solution)/shard_map/convert_element_type | solution.py:30
  229.6 187.0 %all_to_all.54 = bf16[16,256,1024]{1,0,2:T(8,128)(2,1)} all-to-all(bf16[16,256,1024]{1,0,2:T(8,128)(2,1)S(1)} %get-tuple-element.18), channel_id=1, replica_groups=mesh['expert'=4,'shard'=8] {'shard'}, dimensions={2} | all-to-all | bytes 16777216 | tf_op jit(solution)/shard_map/all_to_all | solution.py:34
  416.6 4.9 all-to-all-start.1
  421.5 23.8 %divide_convert_fusion = bf16[16,1024,256]{2,0,1:T(8,128)(2,1)} fusion(f32[16,1024,256]{2,1,0:T(8,128)} %param.12, f32[16,1024]{0,1:T(8,128)S(1)} %copy-done.2, bf16[16,1024,256]{2,1,0:T(8,128)(2,1)} %param.13), kind=kLoop, calls=%fused_computation.1 | loop fusion | flops 16777216 | bytes 33619968 | tf_op jit(solution)/shard_map/convert_element_type | solution.py:31
  445.3 158.3 %all-to-all-done.1 = bf16[16,256,1024]{1,0,2:T(8,128)(2,1)} async-done(((bf16[16,256,1024]{1,0,2:T(8,128)(2,1)}), bf16[16,256,1024]{1,0,2:T(8,128)(2,1)}, u32[]{:S(2)}, u32[]{:S(2)}) %all-to-all-start.1) | async-done | bytes 8388640 | tf_op jit(solution)/shard_map/all_to_all | solution.py:35
  603.6 5.0 all-to-all-start.2
  608.6 0.0 copy-done.3
  608.7 201.9 %all_gather.6 = bf16[2048,16]{0,1:T(8,128)(2,1)S(1)} all-gather(bf16[256,16]{0,1:T(8,128)(2,1)S(1)} %multiply_convert_fusion), channel_id=1, replica_groups=mesh['expert'=4,'shard'=8] {'shard'}, dimensions={0}, use_global_device_ids=true | all-gather | bytes 73728 | tf_op jit(solution)/shard_map/all_gather | solution.py:48
  810.6 6.0 all_gather.7
  816.5 0.8 constant_dynamic-slice_fusion
  817.4 0.7 copy.40
  818.1 0.7 copy.41
  818.7 0.8 constant_dynamic-slice_fusion.2
  819.6 0.7 copy.39
  820.2 12.3 %copy.32 = bf16[16,8,256,128]{3,2,1,0:T(8,128)(2,1)} copy(bf16[16,8,256,128]{2,0,3,1:T(8,128)(2,1)} %bitcast.15) | data formatting | bytes 16777216 | tf_op jit(solution)/shard_map/all_to_all | solution.py:34
  832.5 12.3 %copy.35 = bf16[16,8,256,128]{3,2,1,0:T(8,128)(2,1)} copy(bf16[16,8,256,128]{2,0,3,1:T(8,128)(2,1)} %bitcast.4) | data formatting | bytes 16777216 | tf_op jit(solution)/shard_map/all_to_all | solution.py:35
  844.8 0.0 all-to-all-done.2
  844.8 11.4 %copy.38 = bf16[16,128,8,256]{3,2,1,0:T(8,128)(2,1)} copy(bf16[16,128,8,256]{3,0,1,2:T(8,128)(2,1)} %bitcast.7) | data formatting | bytes 16777216 | tf_op jit(solution)/shard_map/all_to_all | solution.py:37
  856.2 13.4 %all_to_all.50 = bf16[16,128,2048]{2,1,0:T(8,128)(2,1)} reshape(bf16[16,128,8,256]{3,2,1,0:T(8,128)(2,1)} %copy.38) | data formatting | bytes 16777216 | tf_op jit(solution)/shard_map/all_to_all | solution.py:37
  869.6 0.7 copy.53
  (13 shorter events, 0.0 us)
Async XLA Ops:
  7.2 201.8 %all-reduce.3.cloned.1.call-start = ((), (), s32[]{:S(2)}) async-start(), calls=%async_computation.3 | async-start | bytes 3145728 | tf_op jit(solution)/shard_map/pmax | solution.py:20
  67.4 13.2 %copy-start = (f32[16,256,1024]{1,0,2:T(8,128)S(1)}, f32[16,256,1024]{1,0,2:T(8,128)}, u32[]{:S(2)}) copy-start(f32[16,256,1024]{1,0,2:T(8,128)} %copy.31) | copy-start | bytes 50331652
  67.4 15.6 %copy-start.1 = (bf16[16,256,1024]{1,0,2:T(8,128)(2,1)S(1)}, bf16[16,256,1024]{1,0,2:T(8,128)(2,1)}, u32[]{:S(2)}) copy-start(bf16[16,256,1024]{1,0,2:T(8,128)(2,1)} %copy.30) | copy-start | bytes 25165828
  67.4 19.9 %slice-start = ((s8[8388608]{0:T(1024)(128)(4,1)}), s8[4194304]{0:T(1024)(128)(4,1)S(1)}, s32[]{:S(2)}) async-start(s8[8388608]{0:T(1024)(128)(4,1)} %bitcast.13), calls=%async_computation.4 | async-start | bytes 8388608
  83.0 4.3 slice-start.1
  229.6 192.0 %copy-start.2 = (f32[16,1024]{0,1:T(8,128)S(1)}, f32[16,1024]{0,1:T(8,128)}, u32[]{:S(2)}) copy-start(f32[16,1024]{0,1:T(8,128)} %get-tuple-element.16) | copy-start | bytes 196612
  416.6 187.0 %all-to-all-start.1 = ((bf16[16,256,1024]{1,0,2:T(8,128)(2,1)}), bf16[16,256,1024]{1,0,2:T(8,128)(2,1)}, u32[]{:S(2)}, u32[]{:S(2)}) async-start(bf16[16,256,1024]{1,0,2:T(8,128)(2,1)} %get-tuple-element.17), calls=%async_computation.1 | async-start | bytes 16777216 | tf_op jit(solution)/shard_map/all_to_all | solution.py:35
  445.3 163.3 %copy-start.3 = (f32[256,16]{0,1:T(8,128)S(1)}, f32[256,16]{0,1:T(8,128)}, u32[]{:S(2)}) copy-start(f32[256,16]{0,1:T(8,128)} %param.14) | copy-start | bytes 49156
  445.3 163.3 %copy-start.4 = (f32[256]{0:T(256)S(1)}, f32[256]{0:T(256)}, u32[]{:S(2)}) copy-start(f32[256]{0:T(256)} %param.15) | copy-start | bytes 3076
  603.6 241.2 %all-to-all-start.2 = ((bf16[16,1024,256]{2,0,1:T(8,128)(2,1)}), bf16[16,1024,256]{2,0,1:T(8,128)(2,1)}, u32[]{:S(2)}, u32[]{:S(2)}) async-start(bf16[16,1024,256]{2,0,1:T(8,128)(2,1)} %divide_convert_fusion), calls=%async_computation.2 | async-start | bytes 16777216 | tf_op jit(solution)/shard_map/all_to_all | solution.py:37
Sparse Core Ops, SparseCore 0:
  116.7 92.2 all-reduce.2
where the time goes:
time: 880 us; the launch traced here: 877 us
  blocking collectives  395 us (45%)
  waiting for transfers between devices  251 us (29%)
  local copies, waits for them, and re-layouts  118 us (13%)
  other arithmetic  88.9 us (10%)
  between operations  14.1 us (2%)
  starting transfers between devices  10 us (1%)
    all_gather x1, blocking collectives, per_device(): row_router = lax.all_gather(part_router, 'shard', axis=0, tiled=True)  202 us
    all_to_all x1, blocking collectives, per_device(): lax.all_to_all(narrow_gate, 'shard', split_axis=2, concat_axis=1, tiled=T...  187 us
    all_to_all x1, waiting for transfers between devices, per_device(): lax.all_to_all(narrow_up, 'shard', split_axis=2, concat_axis=1, tiled=True)  158 us
    pmax x1, waiting for transfers between devices, per_device(): lax.pmax((jnp.max(jnp.abs(merged_gate), axis=1), jnp.max(jnp.abs(merged_u...  92.5 us
    unnamed x22, local copies, waits for them, and re-layouts  67.4 us
    reduce_max x1, other arithmetic, per_device(): jnp.max(jnp.abs(merged_down), axis=2)  29.3 us
    all_to_all x2, local copies, waits for them, and re-layouts, per_device(): lax.all_to_all(narrow_down, 'shard', split_axis=1, concat_axis=2, tiled=T...  24.8 us
    convert_element_type x1, other arithmetic, per_device(): (merged_down / jnp.expand_dims(scale_down, 2)).astype(jnp.bfloat16)  23.8 us
  transfers between devices with their start and end apart: 3, of which 2 were waited for; matrix products, arithmetic and copies ran while one was open for 6% of the time, Pallas kernels for 0%

commit v1 on v0

--- a/solution.py
+++ b/solution.py
@@ -31,7 +31,12 @@
         (merged_down / jnp.expand_dims(scale_down, 2)).astype(jnp.bfloat16),
     )
     final_gate, final_up = (
-        lax.all_to_all(narrow_gate, "shard", split_axis=2, concat_axis=1, tiled=True),
+        jnp.concatenate(
+            lax.all_to_all(
+                jnp.stack(jnp.split(narrow_gate, lax.axis_size("shard"), axis=2)), "shard", 0, 0
+            ),
+            axis=1,
+        ),
         lax.all_to_all(narrow_up, "shard", split_axis=2, concat_axis=1, tiled=True),
     )
     final_down = lax.all_to_all(narrow_down, "shard", split_axis=1, concat_axis=2, tiled=True)

time: 880 us -> 822 us (0.934)
  blocking collectives: 395 us -> 208 us
  waiting for transfers between devices: 251 us -> 405 us
  local copies, waits for them, and re-layouts: 118 us -> 88.9 us
    all_to_all x1 -> x0, blocking collectives: 187 us -> none  [per_device(): lax.all_to_all(narrow_gate, 'shard', split_axis=2, concat_axis=1, tiled=T...]
    all_to_all x1, waiting for transfers between devices: 0.01 us -> 163 us  [per_device(): lax.all_to_all(narrow_down, 'shard', split_axis=1, concat_axis=2, tiled=T...]
    unnamed x22 -> x34, local copies, waits for them, and re-layouts: 67.4 us -> 41.2 us
    all_to_all x1 -> x0, local copies, waits for them, and re-layouts: 12.3 us -> none  [per_device(): lax.all_to_all(narrow_gate, 'shard', split_axis=2, concat_axis=1, tiled=T...]
    pmax x1, waiting for transfers between devices: 92.5 us -> 82.4 us  [per_device(): lax.pmax((jnp.max(jnp.abs(merged_gate), axis=1), jnp.max(jnp.abs(merged_u...]
    convert_element_type x0 -> x1, other arithmetic: none -> 9.39 us  [per_device(): (merged_gate / jnp.expand_dims(scale_gate, 1)).astype(jnp.bfloat16)]
  transfers between devices with their start and end apart: 3 -> 4, of which waited for: 2 -> 3; matrix products, arithmetic and copies ran while one was open for 6% -> 8% of each run, Pallas kernels for 0% -> 0%
where the time goes in v1:
time: 822 us; the launch traced here: 821 us
  waiting for transfers between devices  405 us (49%)
  blocking collectives  208 us (25%)
  other arithmetic  89.9 us (11%)
  local copies, waits for them, and re-layouts  88.9 us (11%)
  starting transfers between devices  15.2 us (2%)
  between operations  14.2 us (2%)
    all_gather x1, blocking collectives, per_device(): row_router = lax.all_gather(part_router, 'shard', axis=0, tiled=True)  202 us
    all_to_all x1, waiting for transfers between devices, per_device(): lax.all_to_all(narrow_down, 'shard', split_axis=1, concat_axis=2, tiled=T...  163 us
    all_to_all x1, waiting for transfers between devices, per_device(): lax.all_to_all(narrow_up, 'shard', split_axis=2, concat_axis=1, tiled=True)  159 us
    pmax x1, waiting for transfers between devices, per_device(): lax.pmax((jnp.max(jnp.abs(merged_gate), axis=1), jnp.max(jnp.abs(merged_u...  82.4 us
    unnamed x34, local copies, waits for them, and re-layouts  41.2 us
    reduce_max x1, other arithmetic, per_device(): jnp.max(jnp.abs(merged_down), axis=2)  30.1 us
    all_to_all x2, local copies, waits for them, and re-layouts, per_device(): lax.all_to_all(narrow_down, 'shard', split_axis=1, concat_axis=2, tiled=T...  24.8 us
    convert_element_type x1, other arithmetic, per_device(): (merged_down / jnp.expand_dims(scale_down, 2)).astype(jnp.bfloat16)  23.8 us
  transfers between devices with their start and end apart: 4, of which 3 were waited for; matrix products, arithmetic and copies ran while one was open for 8% of the time, Pallas kernels for 0%

profile of v1, /device:TPU:0, one launch (start us, length us, event | category | flops | bytes accessed | tf_op | source)
XLA Modules:
  0.0 820.9 jit_solution(3521776614506022651)
XLA Ops:
  7.2 12.5 %copy.28 = bf16[16,256,1024]{1,0,2:T(8,128)(2,1)} copy(bf16[16,256,1024]{2,1,0:T(8,128)(2,1)} %param.11) | data formatting | bytes 16777216 | tf_op args[3]
  19.7 17.6 %copy.29 = f32[16,256,1024]{1,0,2:T(8,128)} copy(f32[16,256,1024]{2,1,0:T(8,128)} %param.10) | data formatting | bytes 33554432 | tf_op args[2]
  37.3 10.3 %abs_reduce_fusion.2 = f32[16,1024]{1,0:T(8,128)} fusion(f32[16,256,1024]{2,1,0:T(8,128)} %param.8, bf16[16,256,1024]{2,1,0:T(8,128)(2,1)} %param.9), kind=kLoop, calls=%fused_computation.7 | loop fusion | flops 16760832 | bytes 25231360 | tf_op jit(solution)/shard_map/reduce_max | solution.py:22
  47.9 30.1 %abs_reduce_fusion = f32[16,1024]{0,1:T(8,128)} fusion(f32[16,1024,256]{2,1,0:T(8,128)} %param.12, bf16[16,1024,256]{2,1,0:T(8,128)(2,1)S(1)} %copy-done), kind=kLoop, calls=%fused_computation.2 | loop fusion | flops 16760832 | bytes 25231360 | tf_op jit(solution)/shard_map/reduce_max | solution.py:24
  78.1 4.3 abs_reduce_fusion.1
  82.4 82.4 %all-reduce.3.cloned.1.call-done = (f32[16,1024]{1,0:T(8,128)}, f32[16,1024]{0,1:T(8,128)}, f32[16,1024]{0,1:T(8,128)}) async-done(((f32[16,1024]{1,0:T(8,128)}, f32[16,1024]{0,1:T(8,128)}, f32[16,1024]{0,1:T(8,128)}), (f32[16,1024]{1,0:T(8,128)}, f32[16,1024]{0,1:T(8,128)}, f32[16,1024]{0,1:T(8,128)})) %all-reduce.3.cloned.1.call-update) | async-done | bytes 196624 | tf_op jit(solution)/shard_map/pmax | solution.py:20
  164.8 12.1 %divide_convert_fusion.1 = bf16[16,256,1024]{1,0,2:T(8,128)(2,1)} fusion(f32[16,256,1024]{1,0,2:T(8,128)} %copy.29, bf16[16,256,1024]{1,0,2:T(8,128)(2,1)} %copy.28, f32[16,1024]{0,1:T(8,128)} %get-tuple-element.15), kind=kLoop, calls=%fused_computation.3 | loop fusion | flops 16777216 | bytes 33619968 | tf_op jit(solution)/shard_map/convert_element_type | solution.py:30
  176.9 5.3 all-to-all-start.1
  182.1 23.8 %divide_convert_fusion = bf16[16,1024,256]{2,0,1:T(8,128)(2,1)} fusion(f32[16,1024,256]{2,1,0:T(8,128)} %param.12, f32[16,1024]{0,1:T(8,128)S(1)} %copy-done.1, bf16[16,1024,256]{2,1,0:T(8,128)(2,1)} %param.13), kind=kLoop, calls=%fused_computation.1 | loop fusion | flops 16777216 | bytes 33619968 | tf_op jit(solution)/shard_map/convert_element_type | solution.py:31
  205.9 159.2 %all-to-all-done.1 = bf16[16,256,1024]{1,0,2:T(8,128)(2,1)} async-done(((bf16[16,256,1024]{1,0,2:T(8,128)(2,1)}), bf16[16,256,1024]{1,0,2:T(8,128)(2,1)}, u32[]{:S(2)}, u32[]{:S(2)}) %all-to-all-start.1) | async-done | bytes 8388640 | tf_op jit(solution)/shard_map/all_to_all | solution.py:40
  365.2 5.0 all-to-all-start.2
  370.2 9.4 %divide_convert_fusion.2 = bf16[16,256,1024]{2,1,0:T(8,128)(2,1)S(1)} fusion(f32[16,256,1024]{2,1,0:T(8,128)} %param.8, bf16[16,256,1024]{2,1,0:T(8,128)(2,1)} %param.9, f32[16,1024]{1,0:T(8,128)S(1)} %copy-done.2), kind=kLoop, calls=%fused_computation.6 | loop fusion | flops 16777216 | bytes 33619968 | tf_op jit(solution)/shard_map/convert_element_type | solution.py:29
  379.6 1.2 fusion.7
  380.8 1.2 fusion.6
  382.1 1.2 fusion.5
  383.3 1.2 fusion.4
  384.6 1.2 fusion.3
  385.8 1.2 fusion.2
  387.0 1.2 fusion.1
  388.3 1.2 fusion
  389.5 163.0 %all-to-all-done.2 = bf16[16,1024,256]{2,0,1:T(8,128)(2,1)} async-done(((bf16[16,1024,256]{2,0,1:T(8,128)(2,1)}), bf16[16,1024,256]{2,0,1:T(8,128)(2,1)}, u32[]{:S(2)}, u32[]{:S(2)}) %all-to-all-start.2) | async-done | bytes 8388640 | tf_op jit(solution)/shard_map/all_to_all | solution.py:42
  552.6 5.0 all-to-all-start
  557.6 202.0 %all_gather.6 = bf16[2048,16]{0,1:T(8,128)(2,1)S(1)} all-gather(bf16[256,16]{0,1:T(8,128)(2,1)S(1)} %multiply_convert_fusion), channel_id=1, replica_groups=mesh['expert'=4,'shard'=8] {'shard'}, dimensions={0}, use_global_device_ids=true | all-gather | bytes 73728 | tf_op jit(solution)/shard_map/all_gather | solution.py:53
  759.5 6.0 all_gather.7
  765.5 0.8 constant_dynamic-slice_fusion
  766.4 0.7 copy.35
  767.1 0.7 copy.34
  768.3 12.3 %copy.30 = bf16[16,8,256,128]{3,2,1,0:T(8,128)(2,1)} copy(bf16[16,8,256,128]{2,0,3,1:T(8,128)(2,1)} %bitcast.11) | data formatting | bytes 16777216 | tf_op jit(solution)/shard_map/all_to_all | solution.py:40
  780.6 11.4 %copy.33 = bf16[16,128,8,256]{3,2,1,0:T(8,128)(2,1)} copy(bf16[16,128,8,256]{3,0,1,2:T(8,128)(2,1)} %bitcast.14) | data formatting | bytes 16777216 | tf_op jit(solution)/shard_map/all_to_all | solution.py:42
  792.0 13.4 %all_to_all.37 = bf16[16,128,2048]{2,1,0:T(8,128)(2,1)} reshape(bf16[16,128,8,256]{3,2,1,0:T(8,128)(2,1)} %copy.33) | data formatting | bytes 16777216 | tf_op jit(solution)/shard_map/all_to_all | solution.py:42
  805.4 7.9 copy.27
  813.3 0.7 copy.54
  (29 shorter events, 1.0 us)
Async XLA Ops:
  7.2 157.6 %all-reduce.3.cloned.1.call-start = ((), (), s32[]{:S(2)}) async-start(), calls=%async_computation.3 | async-start | bytes 2228224 | tf_op jit(solution)/shard_map/pmax | solution.py:20
  37.3 10.6 %copy-start = (bf16[16,1024,256]{2,1,0:T(8,128)(2,1)S(1)}, bf16[16,1024,256]{2,1,0:T(8,128)(2,1)}, u32[]{:S(2)}) copy-start(bf16[16,1024,256]{2,1,0:T(8,128)(2,1)} %param.13) | copy-start | bytes 25165828
  37.3 40.8 %slice-start = ((s8[16777216]{0:T(1024)(128)(4,1)}), s8[4194304]{0:T(1024)(128)(4,1)S(1)}, s32[]{:S(2)}) async-start(s8[16777216]{0:T(1024)(128)(4,1)} %bitcast.43), calls=%async_computation.4 | async-start | bytes 8388608
  37.3 40.8 %slice-start.1 = ((s8[16777216]{0:T(1024)(128)(4,1)}), s8[4194304]{0:T(1024)(128)(4,1)S(1)}, s32[]{:S(2)}) async-start(s8[16777216]{0:T(1024)(128)(4,1)} %bitcast.43), calls=%async_computation.5 | async-start | bytes 8388608
  37.3 40.8 %slice-start.4 = ((s8[8388608]{0:T(1024)(128)(4,1)}), s8[4194304]{0:T(1024)(128)(4,1)S(1)}, s32[]{:S(2)}) async-start(s8[8388608]{0:T(1024)(128)(4,1)} %bitcast.45), calls=%async_computation.8 | async-start | bytes 8388608
  47.9 30.1 %slice-start.2 = ((s8[16777216]{0:T(1024)(128)(4,1)}), s8[4194304]{0:T(1024)(128)(4,1)S(1)}, s32[]{:S(2)}) async-start(s8[16777216]{0:T(1024)(128)(4,1)} %bitcast.43), calls=%async_computation.6 | async-start | bytes 8388608
  47.9 30.2 %slice-start.3 = ((s8[16777216]{0:T(1024)(128)(4,1)}), s8[4194304]{0:T(1024)(128)(4,1)S(1)}, s32[]{:S(2)}) async-start(s8[16777216]{0:T(1024)(128)(4,1)} %bitcast.43), calls=%async_computation.7 | async-start | bytes 8388608
  47.9 30.2 %slice-start.5 = ((s8[8388608]{0:T(1024)(128)(4,1)}), s8[4194304]{0:T(1024)(128)(4,1)S(1)}, s32[]{:S(2)}) async-start(s8[8388608]{0:T(1024)(128)(4,1)} %bitcast.45), calls=%async_computation.9 | async-start | bytes 8388608
  176.9 5.3 copy-start.1
  176.9 188.3 %all-to-all-start.1 = ((bf16[16,256,1024]{1,0,2:T(8,128)(2,1)}), bf16[16,256,1024]{1,0,2:T(8,128)(2,1)}, u32[]{:S(2)}, u32[]{:S(2)}) async-start(bf16[16,256,1024]{1,0,2:T(8,128)(2,1)} %divide_convert_fusion.1), calls=%async_computation.1 | async-start | bytes 16777216 | tf_op jit(solution)/shard_map/all_to_all | solution.py:40
  205.9 164.2 %copy-start.2 = (f32[16,1024]{1,0:T(8,128)S(1)}, f32[16,1024]{1,0:T(8,128)}, u32[]{:S(2)}) copy-start(f32[16,1024]{1,0:T(8,128)} %get-tuple-element.14) | copy-start | bytes 196612
  365.2 187.4 %all-to-all-start.2 = ((bf16[16,1024,256]{2,0,1:T(8,128)(2,1)}), bf16[16,1024,256]{2,0,1:T(8,128)(2,1)}, u32[]{:S(2)}, u32[]{:S(2)}) async-start(bf16[16,1024,256]{2,0,1:T(8,128)(2,1)} %divide_convert_fusion), calls=%async_computation.2 | async-start | bytes 16777216 | tf_op jit(solution)/shard_map/all_to_all | solution.py:42
  389.5 168.0 %copy-start.3 = (f32[256,16]{0,1:T(8,128)S(1)}, f32[256,16]{0,1:T(8,128)}, u32[]{:S(2)}) copy-start(f32[256,16]{0,1:T(8,128)} %param.14) | copy-start | bytes 49156
  389.5 168.0 %copy-start.4 = (f32[256]{0:T(256)S(1)}, f32[256]{0:T(256)}, u32[]{:S(2)}) copy-start(f32[256]{0:T(256)} %param.15) | copy-start | bytes 3076
  552.6 252.9 %all-to-all-start = ((bf16[8,16,256,128]{3,2,1,0:T(8,128)(2,1)}), bf16[8,16,256,128]{3,2,1,0:T(8,128)(2,1)}, u32[]{:S(2)}, u32[]{:S(2)}) async-start(bf16[8,16,256,128]{3,2,1,0:T(8,128)(2,1)} %fusion), calls=%async_computation | async-start | bytes 16777216 | tf_op jit(solution)/shard_map/all_to_all | solution.py:35
Sparse Core Ops, SparseCore 0:
  82.5 82.2 all-reduce.2
